TPU v7x, 32 devices: a whole 2x2x4 slice. The times are simulated.
32 devices in a mesh: section: 4 (over y, core), dp: 8 (over z, x).
Axes of the slice: x: 2, y: 2, z: 4, core: 2. Of those that a mesh axis runs over, the one named last changes fastest.
Arguments:
- patch_tokens: bfloat16 [4, 8, 196, 1280], P(None, 'dp'), may hold values from -24 to 24
- visible: int32 [4, 8, 98], P(None, 'dp'), may hold values from 0 to 195, as said below
- keep_mask: int32 [4, 8, 98], P(None, 'dp'), may hold values from 0 to 1, as said below
- lengths: int32 [4], replicated, may hold values from 49 to 98
- qkv_weight: bfloat16 [4, 1280, 1920], P('section', 'dp'), may hold values from -4 to 4
- out_weight: bfloat16 [4, 640, 1280], P('section', 'dp'), may hold values from -0.25 to 0.25
- norm_gain: bfloat16 [4, 1280], P('section'), may hold values from 0.099609375 to 1.8984375
- targets: bfloat16 [4, 4, 8, 98, 1280], P('section', None, 'dp'), may hold values from -12 to 12
Outputs:
- hidden_states: bfloat16 [4, 4, 8, 98, 1280], P('section', None, 'dp')
- token_loss: float32 [4, 8, 98], P(None, 'dp')
- loss: float32 [4], replicated
Inputs may be any that keep to these rules, and one draw needn't show every extreme that they name: `visible`: the 98 entries of one image are different patch numbers. `keep_mask`: slot 0 of every image is 1.
All inputs are finite; a program needn't handle non-finite values.
Results may differ from a plain program's by a relative error of at most 0.019.
Values may be sent and summed in bfloat16 or wider, within the bound.
A program may use at most 128 MiB of HBM per device.

v0:
```python
import functools

import jax
import jax.numpy as jnp
from jax import lax
from jax.experimental import pallas as pl
from jax.experimental.pallas import tpu as pltpu
from jax.sharding import PartitionSpec as P

HEADS = 8
HDIM = 80
MESH = pl.DeviceIdType.MESH


def norm_rows(values):
    row_mean = jnp.mean(values, -1, keepdims=True)
    centered = values - row_mean
    variance = jnp.mean(centered * centered, -1, keepdims=True)
    return centered * lax.rsqrt(variance + 1e-06)


def eye_mask(rows, columns):
    shape = (rows, columns)
    return lax.broadcasted_iota(jnp.int32, shape, 0) == lax.broadcasted_iota(jnp.int32, shape, 1)


def to_column(row, rows):
    return jnp.sum(jnp.where(eye_mask(rows, row.shape[1]), row, 0.0), axis=1, keepdims=True)


def to_row(column, columns):
    return jnp.sum(jnp.where(eye_mask(column.shape[0], columns), column, 0.0), axis=0, keepdims=True)


def halves(rows):
    low = (rows // 2 + 15) // 16 * 16
    return ((0, low), (low, rows - low))


def kernel_body(
    gathers, sections, ring_size,
    lengths, patches_in, visible, keep, w_qkv_in, w_out_in, gain, targets_in,
    hidden, token_loss, loss,
    w_qkv_all, w_out_all, x_in, x_out, proj, context, keep_rows, visible_rows,
    errors, error_slots, sums, sum_slots,
    own_sem, ring_send, ring_recv, x_send, x_recv, error_send, error_recv, sum_send, sum_recv, turn_sem, targets_held, targets, targets_sem,
    patches_held, patches, patches_sem, hidden_held, hidden_sem,
):
    section = lax.axis_index("section")
    member = lax.axis_index("dp")
    micro_count, slots = targets.shape[0], targets.shape[1]
    rows = x_in.shape[1]
    width = x_in.shape[2]
    head_width = HEADS * HDIM

    pairs = ((w_qkv_in, w_qkv_all), (w_out_in, w_out_all))
    own_copies = []
    if gathers:
        for which, (shard, whole) in enumerate(pairs):
            own_rows = shard.shape[0]
            target = whole.at[pl.ds(pl.multiple_of(member * own_rows, 16), own_rows)]
            own_copies.append(pltpu.make_async_copy(shard, target, own_sem.at[which]))
            own_copies[-1].start()
    targets_copy = pltpu.make_async_copy(targets_in, targets_held, targets_sem)
    targets_copy.start()
    patches_copy = pltpu.make_async_copy(patches_in, patches_held, patches_sem)

    @pl.when(section == 0)
    def _():
        patches_copy.start()

    barrier = pltpu.get_barrier_semaphore()
    for distance in range(1, ring_size):
        pl.semaphore_signal(
            barrier, inc=1, device_id={"dp": lax.rem(member + distance, ring_size)}, device_id_type=MESH
        )
    for distance in range(1, sections):
        pl.semaphore_signal(
            barrier, inc=1, device_id={"section": lax.rem(section + distance, sections)}, device_id_type=MESH
        )
    pl.semaphore_wait(barrier, ring_size - 1 + sections - 1)

    def prepare():
        keep_rows[...] = jnp.zeros_like(keep_rows)
        visible_rows[...] = jnp.full(visible_rows.shape, -1.0, jnp.float32)
        keep_rows[:, :, 0:slots] = keep[...].astype(jnp.float32)
        visible_rows[:, :, 0:slots] = visible[...].astype(jnp.float32)

        targets_copy.wait()
        for m in range(micro_count):
            targets[m] = targets_held[:, m, :].astype(jnp.float32)

        @pl.when(section == 0)
        def _():
            patches_copy.wait()
            for m in range(micro_count):
                patches[m] = patches_held[:, m, :]

            def pick(m, carry):
                chosen = to_column(visible_rows[m], rows)
                patch_pos = lax.broadcasted_iota(jnp.int32, (rows, patches.shape[1]), 1).astype(jnp.float32)
                one_hot = jnp.where(patch_pos == chosen, 1.0, 0.0).astype(jnp.bfloat16)
                x_in[m] = jnp.dot(
                    one_hot, patches[m], preferred_element_type=jnp.float32
                ).astype(jnp.bfloat16)
                return carry

            lax.fori_loop(0, micro_count, pick, 0)

    if gathers:
        half = ring_size // 2
        column, line = lax.rem(member, 2), member // 2
        place = line + column * (ring_size - 1 - 2 * line)

        def device_at(position):
            position = lax.rem(position + 2 * ring_size, ring_size)
            far = position // half
            return 2 * position * (1 - far) + far * (2 * (ring_size - 1 - position) + 1)

        pieces = [(which, part) for part in (0, 1) for which in (0, 1)]

        def span(which, part, owner):
            shard_rows = pairs[which][0].shape[0]
            start, count = halves(shard_rows)[part]
            return pl.ds(pl.multiple_of(owner * shard_rows + start, 16), count)

        def hop(way, step, which, part, owner):
            there = pairs[which][1].at[span(which, part, owner)]
            index = ((way * half + step) * 2 + which) * 2 + part
            return pltpu.make_async_remote_copy(
                src_ref=there, dst_ref=there,
                send_sem=ring_send.at[index], recv_sem=ring_recv.at[index],
                device_id={"dp": device_at(place + 1 - 2 * way)}, device_id_type=MESH,
            )

        started = []

        def wanted(way, step):
            return [(w, p) for w, p in pieces if step < half - 1 or p == way]

        first = [
            hop(way, 0, w, p, member)
            for w, p in pieces for way in (0, 1) if (w, p) in wanted(way, 0)
        ]
        started.extend(first)
        early = lax.rem(section, 2) == 0
        for copy in own_copies:
            copy.wait()

        @pl.when(early)
        def _():
            for copy in first:
                copy.start()

        prepare()

        @pl.when(jnp.logical_not(early))
        def _():
            pl.semaphore_wait(turn_sem, 1)
            for copy in first:
                copy.start()

        for step in range(half):
            if step == max(half - 2, 0):
                @pl.when(early & (section + 1 < sections))
                def _():
                    pl.semaphore_signal(
                        turn_sem, inc=1, device_id={"section": lax.rem(section + 1, sections)},
                        device_id_type=MESH,
                    )

            for w, p in pieces:
                for way in (0, 1):
                    if (w, p) not in wanted(way, step):
                        continue
                    owner = device_at(place - (1 - 2 * way) * (step + 1))
                    hop(way, step, w, p, owner).wait_recv()
                    if step + 1 < half and (w, p) in wanted(way, step + 1):
                        copy = hop(way, step + 1, w, p, owner)
                        copy.start()
                        started.append(copy)
        w_qkv, w_out = w_qkv_all, w_out_all
    else:
        prepare()
        started = []
        w_qkv, w_out = w_qkv_in, w_out_in

    def pass_on(m):
        return pltpu.make_async_remote_copy(
            src_ref=x_out.at[m], dst_ref=x_in.at[m],
            send_sem=x_send.at[m], recv_sem=x_recv.at[m],
            device_id={"section": lax.rem(section + 1, sections)}, device_id_type=MESH,
        )

    def live_row(m):
        slot = lax.broadcasted_iota(jnp.int32, (1, rows), 1)
        return (keep_rows[m] > 0.5) & (slot < lengths[m])

    def layer(m, carry):
        @pl.when(section > 0)
        def _():
            pass_on(m).wait_recv()

        live = live_row(m)
        tokens = x_in[m].astype(jnp.float32)
        normed = (norm_rows(tokens) * gain[...].astype(jnp.float32)).astype(jnp.bfloat16)
        total = 3 * head_width
        for start in range(0, total, 256):
            stop = min(start + 256, total)
            proj[:, start:stop] = jnp.dot(
                normed, w_qkv[:, start:stop], preferred_element_type=jnp.float32
            ).astype(jnp.bfloat16)
        context[...] = jnp.zeros_like(context)
        for head in range(HEADS):
            low, high = head * HDIM, (head + 1) * HDIM
            left, right = low // 128 * 128, -(-high // 128) * 128
            lane = lax.broadcasted_iota(jnp.int32, (1, right - left), 1) + left
            inside = jnp.where((lane >= low) & (lane < high), 1.0, 0.0).astype(jnp.bfloat16)
            queries = proj[:, left:right] * inside
            key_rows = proj[:, head_width + left:head_width + right]
            value_rows = proj[:, 2 * head_width + left:2 * head_width + right] * inside
            scores = lax.dot_general(
                queries, key_rows, (((1,), (1,)), ((), ())), preferred_element_type=jnp.float32
            ) * HDIM ** (-0.5)
            scores = jnp.where(live, scores, -1e30)
            weights = jnp.exp(scores - jnp.max(scores, -1, keepdims=True))
            shares = (weights / jnp.sum(weights, -1, keepdims=True)).astype(jnp.bfloat16)
            context[:, left:right] += jnp.dot(shares, value_rows, preferred_element_type=jnp.float32)
        mixed = context[...].astype(jnp.bfloat16)
        for start in range(0, width, 256):
            stop = min(start + 256, width)
            x_out[m, :, start:stop] = (
                x_in[m, :, start:stop].astype(jnp.float32)
                + jnp.dot(mixed, w_out[:, start:stop], preferred_element_type=jnp.float32)
            ).astype(jnp.bfloat16)

        @pl.when(section < sections - 1)
        def _():
            pass_on(m).start()

        output = x_out[m].astype(jnp.float32)
        live_value = jnp.where(live, 1.0, 0.0)
        live_column = to_column(live_value, rows) > 0.5
        hidden_held[m] = jnp.where(live_column, output, 0.0)[0:slots].astype(jnp.bfloat16)
        pltpu.make_async_copy(hidden_held.at[m], hidden.at[m], hidden_sem.at[m]).start()
        deviation = norm_rows(output)[0:slots] - targets[m]
        error = jnp.mean(deviation * deviation, -1, keepdims=True)
        errors[m] = jnp.where(live, to_row(error, rows), 0.0)
        sums[micro_count + m] = jnp.broadcast_to(
            jnp.sum(live_value, axis=1, keepdims=True), (1, sums.shape[2])
        )
        return carry

    lax.fori_loop(0, micro_count, layer, 0)

    def error_copy(distance, slot, peer):
        return pltpu.make_async_remote_copy(
            src_ref=errors, dst_ref=error_slots.at[slot],
            send_sem=error_send.at[distance], recv_sem=error_recv.at[distance],
            device_id={"section": peer}, device_id_type=MESH,
        )

    for distance in range(1, sections):
        copy = error_copy(distance, section, lax.rem(section + distance, sections))
        copy.start()
        started.append(copy)
    error_slots[section] = errors[...]
    for distance in range(1, sections):
        sender = lax.rem(section + sections - distance, sections)
        error_copy(distance, sender, sender).wait_recv()
    error_total = error_slots[0]
    for other in range(1, sections):
        error_total = error_total + error_slots[other]
    token_loss[...] = error_total[:, :, 0:slots]
    sums[0:micro_count] = jnp.broadcast_to(
        jnp.sum(error_total, axis=2, keepdims=True), (micro_count, 1, sums.shape[2])
    )

    def sum_copy(distance, slot, peer):
        return pltpu.make_async_remote_copy(
            src_ref=sums, dst_ref=sum_slots.at[slot],
            send_sem=sum_send.at[distance], recv_sem=sum_recv.at[distance],
            device_id={"dp": peer}, device_id_type=MESH,
        )

    for distance in range(1, ring_size):
        copy = sum_copy(distance, member, lax.rem(member + distance, ring_size))
        copy.start()
        started.append(copy)
    sum_slots[member] = sums[...]
    for distance in range(1, ring_size):
        sender = lax.rem(member + ring_size - distance, ring_size)
        sum_copy(distance, sender, sender).wait_recv()
    total_sums = sum_slots[0]
    for other in range(1, ring_size):
        total_sums = total_sums + sum_slots[other]
    loss[...] = total_sums[0:micro_count] / total_sums[micro_count:2 * micro_count]

    for copy in started:
        copy.wait_send()
    for m in range(micro_count):
        pltpu.make_async_copy(hidden_held.at[m], hidden.at[m], hidden_sem.at[m]).wait()

    @pl.when(section < sections - 1)
    def _():
        for m in range(micro_count):
            pass_on(m).wait_send()


def per_device(
    patch_tokens, visible, keep_mask, lengths, qkv_weight, out_weight, norm_gain, targets
):
    sections, ring_size = lax.axis_size("section"), lax.axis_size("dp")
    micro_count, _, slots = visible.shape
    patch_count, width = patch_tokens.shape[2:]
    rows = -(-slots // 16) * 16
    w_qkv, w_out = qkv_weight[0], out_weight[0]
    gathers = ring_size % 2 == 0 and w_qkv.shape[0] % 32 == 0 and w_out.shape[0] % 16 == 0
    if not gathers:
        w_qkv = lax.all_gather(w_qkv, "dp", axis=0, tiled=True)
        w_out = lax.all_gather(w_out, "dp", axis=0, tiled=True)
    full_qkv = (width, w_qkv.shape[1]) if gathers else (16, 128)
    full_out = (HEADS * HDIM, width) if gathers else (16, 128)
    vmem = pl.BlockSpec(memory_space=pltpu.VMEM)
    hbm = pl.BlockSpec(memory_space=pltpu.HBM)
    shards = hbm if gathers else vmem
    dma = pltpu.SemaphoreType.DMA
    hidden, token_loss, loss = pl.pallas_call(
        functools.partial(kernel_body, gathers, sections, ring_size),
        out_shape=(
            jax.ShapeDtypeStruct((micro_count, slots, width), jnp.bfloat16),
            jax.ShapeDtypeStruct((micro_count, 1, slots), jnp.float32),
            jax.ShapeDtypeStruct((micro_count, 1, 128), jnp.float32),
        ),
        in_specs=[pl.BlockSpec(memory_space=pltpu.SMEM), hbm, vmem, vmem, shards, shards, vmem, hbm],
        out_specs=(hbm, vmem, vmem),
        scratch_shapes=[
            pltpu.VMEM(full_qkv, jnp.bfloat16),
            pltpu.VMEM(full_out, jnp.bfloat16),
            pltpu.VMEM((micro_count, rows, width), jnp.bfloat16),
            pltpu.VMEM((micro_count, rows, width), jnp.bfloat16),
            pltpu.VMEM((rows, 3 * HEADS * HDIM), jnp.bfloat16),
            pltpu.VMEM((rows, HEADS * HDIM), jnp.float32),
            pltpu.VMEM((micro_count, 1, rows), jnp.float32),
            pltpu.VMEM((micro_count, 1, rows), jnp.float32),
            pltpu.VMEM((micro_count, 1, rows), jnp.float32),
            pltpu.VMEM((sections, micro_count, 1, rows), jnp.float32),
            pltpu.VMEM((2 * micro_count, 1, 128), jnp.float32),
            pltpu.VMEM((ring_size, 2 * micro_count, 1, 128), jnp.float32),
            dma((2,)),
            dma((4 * ring_size,)),
            dma((4 * ring_size,)),
            dma((micro_count,)),
            dma((micro_count,)),
            dma((sections,)),
            dma((sections,)),
            dma((ring_size,)),
            dma((ring_size,)),
            pltpu.SemaphoreType.REGULAR,
            pltpu.VMEM((slots, micro_count, width), jnp.bfloat16),
            pltpu.VMEM((micro_count, slots, width), jnp.float32),
            dma,
            pltpu.VMEM((patch_count, micro_count, width), jnp.bfloat16),
            pltpu.VMEM((micro_count, patch_count, width), jnp.bfloat16),
            dma,
            pltpu.VMEM((micro_count, slots, width), jnp.bfloat16),
            dma((micro_count,)),
        ],
        compiler_params=pltpu.CompilerParams(
            collective_id=0, has_side_effects=True, vmem_limit_bytes=67043328
        ),
    )(
        lengths, jnp.transpose(patch_tokens[:, 0], (1, 0, 2)), visible, keep_mask, w_qkv, w_out, norm_gain,
        jnp.transpose(targets[0, :, 0], (1, 0, 2)),
    )
    return (hidden[None, :, None], token_loss, loss[:, 0, 0])


def solution(mesh):
    placed = (
        P(None, "dp", None, None),
        P(None, "dp", None),
        P(None, "dp", None),
        P(),
        P("section", "dp", None),
        P("section", "dp", None),
        P("section", None),
        P("section", None, "dp", None, None),
    )
    return jax.shard_map(
        per_device,
        mesh=mesh,
        in_specs=placed,
        out_specs=(P("section", None, "dp", None, None), P(None, "dp", None), P()),
        check_vma=False,
    )
```

profile of v0, /device:TPU:0, one launch (start us, length us, event | category | flops | bytes accessed | tf_op | source)
XLA Modules:
  0.0 104.8 jit_solution(114973305525729135)
XLA Ops:
  0.6 100.4 %shard_map.103 = (bf16[4,98,1280]{2,1,0:T(8,128)(2,1)}, f32[4,1,98]{2,1,0:T(1,128)}, f32[4,1,128]{2,1,0:T(1,128)}) custom-call(s32[4]{0:T(128)} %lengths.1, bf16[196,4,1280]{2,1,0:T(4,128)(2,1)} %bitcast.9, s32[4,1,98]{2,1,0:T(1,128)} %visible.1, s32[4,1,98]{2,1,0:T(1,128)} %keep.1, bf16[160,1920]{1,0:T(8,128)(2,1)} %bitcast.12, bf16[80,1280]{1,0:T(8,128)(2,1)} %bitcast.13, ...), custom_call_target="tpu_custom_call" | custom-call | tf_op jit(solution)/shard_map/pallas_call | solution.py:328
  101.0 0.0 copy-start
  101.0 0.0 copy-start.1
  101.0 2.6 %copy.12 = bf16[1,4,1,98,1280]{4,1,3,2,0:T(4,128)(2,1)} copy(bf16[1,4,1,98,1280]{4,3,1,2,0:T(8,128)(2,1)} %bitcast.10) | data formatting | bytes 2007040
  103.6 0.0 copy-done
  103.6 0.6 slice_reduce_fusion
  104.2 0.0 copy-done.1
  104.2 0.6 copy.14
Async XLA Ops:
  101.0 2.6 %copy-start = (f32[4,1,128]{2,1,0:T(1,128)S(1)}, f32[4,1,128]{2,1,0:T(1,128)}, u32[]{:S(2)}) copy-start(f32[4,1,128]{2,1,0:T(1,128)} %get-tuple-element.8) | copy-start | bytes 6148
  101.0 3.2 %copy-start.1 = (f32[4,1,98]{2,1,0:T(1,128)S(1)}, f32[4,1,98]{2,1,0:T(1,128)}, u32[]{:S(2)}) copy-start(f32[4,1,98]{2,1,0:T(1,128)} %get-tuple-element.19) | copy-start | bytes 4708
where the time goes:
time: 105 us
  Pallas kernels  100 us (95%)
  local copies, waits for them, and re-layouts  3.78 us (4%)
    pallas_call x1, Pallas kernels, per_device(): pl.pallas_call(functools.partial(kernel_body, gathers, sections, ring_siz...  100 us
    unnamed x6, local copies, waits for them, and re-layouts  3.16 us

commit v1 on v0

--- a/solution.py
+++ b/solution.py
@@ -69,16 +69,27 @@
     def _():
         patches_copy.start()
 
+    half = ring_size // 2
+    column, line = lax.rem(member, 2), member // 2
+    place = line + column * (ring_size - 1 - 2 * line)
+
+    def device_at(position):
+        position = lax.rem(position + 2 * ring_size, ring_size)
+        far = position // half
+        return 2 * position * (1 - far) + far * (2 * (ring_size - 1 - position) + 1)
+
     barrier = pltpu.get_barrier_semaphore()
-    for distance in range(1, ring_size):
-        pl.semaphore_signal(
-            barrier, inc=1, device_id={"dp": lax.rem(member + distance, ring_size)}, device_id_type=MESH
-        )
+    if gathers:
+        greeted = [device_at(place + 1), device_at(place - 1)][:ring_size - 1]
+    else:
+        greeted = [lax.rem(member + distance, ring_size) for distance in range(1, ring_size)]
+    for peer in greeted:
+        pl.semaphore_signal(barrier, inc=1, device_id={"dp": peer}, device_id_type=MESH)
     for distance in range(1, sections):
         pl.semaphore_signal(
             barrier, inc=1, device_id={"section": lax.rem(section + distance, sections)}, device_id_type=MESH
         )
-    pl.semaphore_wait(barrier, ring_size - 1 + sections - 1)
+    pl.semaphore_wait(barrier, len(greeted) + sections - 1)
 
     def prepare():
         keep_rows[...] = jnp.zeros_like(keep_rows)
@@ -108,15 +119,6 @@
             lax.fori_loop(0, micro_count, pick, 0)
 
     if gathers:
-        half = ring_size // 2
-        column, line = lax.rem(member, 2), member // 2
-        place = line + column * (ring_size - 1 - 2 * line)
-
-        def device_at(position):
-            position = lax.rem(position + 2 * ring_size, ring_size)
-            far = position // half
-            return 2 * position * (1 - far) + far * (2 * (ring_size - 1 - position) + 1)
-
         pieces = [(which, part) for part in (0, 1) for which in (0, 1)]
 
         def span(which, part, owner):

time: 105 us -> 105 us (level)
  no operation moved by 1% of the time
where the time goes in v1:
time: 105 us
  Pallas kernels  100 us (95%)
  local copies, waits for them, and re-layouts  3.78 us (4%)
    pallas_call x1, Pallas kernels, per_device(): pl.pallas_call(functools.partial(kernel_body, gathers, sections, ring_siz...  100 us
    unnamed x6, local copies, waits for them, and re-layouts  3.16 us

profile of v1, /device:TPU:0, one launch (start us, length us, event | category | flops | bytes accessed | tf_op | source)
XLA Modules:
  0.0 104.7 jit_solution(4527472668833467024)
XLA Ops:
  0.6 100.3 %shard_map.103 = (bf16[4,98,1280]{2,1,0:T(8,128)(2,1)}, f32[4,1,98]{2,1,0:T(1,128)}, f32[4,1,128]{2,1,0:T(1,128)}) custom-call(s32[4]{0:T(128)} %lengths.1, bf16[196,4,1280]{2,1,0:T(4,128)(2,1)} %bitcast.9, s32[4,1,98]{2,1,0:T(1,128)} %visible.1, s32[4,1,98]{2,1,0:T(1,128)} %keep.1, bf16[160,1920]{1,0:T(8,128)(2,1)} %bitcast.12, bf16[80,1280]{1,0:T(8,128)(2,1)} %bitcast.13, ...), custom_call_target="tpu_custom_call" | custom-call | tf_op jit(solution)/shard_map/pallas_call | solution.py:330
  100.9 0.0 copy-start
  101.0 0.0 copy-start.1
  101.0 2.6 %copy.12 = bf16[1,4,1,98,1280]{4,1,3,2,0:T(4,128)(2,1)} copy(bf16[1,4,1,98,1280]{4,3,1,2,0:T(8,128)(2,1)} %bitcast.10) | data formatting | bytes 2007040
  103.5 0.0 copy-done
  103.5 0.6 slice_reduce_fusion
  104.2 0.0 copy-done.1
  104.2 0.6 copy.14
Async XLA Ops:
  100.9 2.6 %copy-start = (f32[4,1,128]{2,1,0:T(1,128)S(1)}, f32[4,1,128]{2,1,0:T(1,128)}, u32[]{:S(2)}) copy-start(f32[4,1,128]{2,1,0:T(1,128)} %get-tuple-element.8) | copy-start | bytes 6148
  101.0 3.2 %copy-start.1 = (f32[4,1,98]{2,1,0:T(1,128)S(1)}, f32[4,1,98]{2,1,0:T(1,128)}, u32[]{:S(2)}) copy-start(f32[4,1,98]{2,1,0:T(1,128)} %get-tuple-element.19) | copy-start | bytes 4708

commit v2 on v1

--- a/solution.py
+++ b/solution.py
@@ -45,6 +45,7 @@
     errors, error_slots, sums, sum_slots,
     own_sem, ring_send, ring_recv, x_send, x_recv, error_send, error_recv, sum_send, sum_recv, turn_sem, targets_held, targets, targets_sem,
     patches_held, patches, patches_sem, hidden_held, hidden_sem,
+    w_before, mixed_all, mixed_in, x_before, before_send, before_recv, mixed_send, mixed_recv, skip_send, skip_recv,
 ):
     section = lax.axis_index("section")
     member = lax.axis_index("dp")
@@ -53,10 +54,13 @@
     width = x_in.shape[2]
     head_width = HEADS * HDIM
 
-    pairs = ((w_qkv_in, w_qkv_all), (w_out_in, w_out_all))
+    pairs = ((w_qkv_in, w_qkv_all), (w_out_in, w_out_all), (w_out_in, w_before))
+    giver = sections // 2 - 1 if gathers and sections % 2 == 0 and sections >= 4 else -2
+    taker = giver + 1
+    gives, takes = section == giver, section == taker
     own_copies = []
     if gathers:
-        for which, (shard, whole) in enumerate(pairs):
+        for which, (shard, whole) in enumerate(pairs[:2]):
             own_rows = shard.shape[0]
             target = whole.at[pl.ds(pl.multiple_of(member * own_rows, 16), own_rows)]
             own_copies.append(pltpu.make_async_copy(shard, target, own_sem.at[which]))
@@ -91,6 +95,19 @@
         )
     pl.semaphore_wait(barrier, len(greeted) + sections - 1)
 
+    def before_copy():
+        own_rows = w_out_in.shape[0]
+        return pltpu.make_async_remote_copy(
+            src_ref=w_out_in, dst_ref=w_before.at[pl.ds(pl.multiple_of(member * own_rows, 16), own_rows)],
+            send_sem=before_send, recv_sem=before_recv,
+            device_id={"section": taker}, device_id_type=MESH,
+        )
+
+    if giver >= 0:
+        @pl.when(gives)
+        def _():
+            before_copy().start()
+
     def prepare():
         keep_rows[...] = jnp.zeros_like(keep_rows)
         visible_rows[...] = jnp.full(visible_rows.shape, -1.0, jnp.float32)
@@ -128,7 +145,7 @@
 
         def hop(way, step, which, part, owner):
             there = pairs[which][1].at[span(which, part, owner)]
-            index = ((way * half + step) * 2 + which) * 2 + part
+            index = ((way * half + step) * 3 + which) * 2 + part
             return pltpu.make_async_remote_copy(
                 src_ref=there, dst_ref=there,
                 send_sem=ring_send.at[index], recv_sem=ring_recv.at[index],
@@ -181,8 +198,33 @@
                         copy = hop(way, step + 1, w, p, owner)
                         copy.start()
                         started.append(copy)
+        relayed = []
+        if giver >= 0:
+            before = [
+                hop(way, 0, 2, p, member)
+                for p in (0, 1) for way in (0, 1) if (1, p) in wanted(way, 0)
+            ]
+            relayed.extend((0, p, way) for p in (0, 1) for way in (0, 1) if (1, p) in wanted(way, 0))
+
+            @pl.when(takes)
+            def _():
+                before_copy().wait_recv()
+                for copy in before:
+                    copy.start()
+                for step in range(half):
+                    for p in (0, 1):
+                        for way in (0, 1):
+                            if (1, p) not in wanted(way, step):
+                                continue
+                            owner = device_at(place - (1 - 2 * way) * (step + 1))
+                            hop(way, step, 2, p, owner).wait_recv()
+                            if step + 1 < half and (1, p) in wanted(way, step + 1):
+                                hop(way, step + 1, 2, p, owner).start()
+                                relayed.append((step + 1, p, way))
+
         w_qkv, w_out = w_qkv_all, w_out_all
     else:
+        relayed = []
         prepare()
         started = []
         w_qkv, w_out = w_qkv_in, w_out_in
@@ -194,14 +236,42 @@
             device_id={"section": lax.rem(section + 1, sections)}, device_id_type=MESH,
         )
 
+    def skip_copy(m):
+        return pltpu.make_async_remote_copy(
+            src_ref=x_out.at[m], dst_ref=x_before.at[m],
+            send_sem=skip_send.at[m], recv_sem=skip_recv.at[m],
+            device_id={"section": taker}, device_id_type=MESH,
+        )
+
+    def mixed_copy(m):
+        return pltpu.make_async_remote_copy(
+            src_ref=mixed_all.at[m], dst_ref=mixed_in.at[m],
+            send_sem=mixed_send.at[m], recv_sem=mixed_recv.at[m],
+            device_id={"section": taker}, device_id_type=MESH,
+        )
+
+    passes = (section < sections - 1) & jnp.logical_not(gives)
+
     def live_row(m):
         slot = lax.broadcasted_iota(jnp.int32, (1, rows), 1)
         return (keep_rows[m] > 0.5) & (slot < lengths[m])
 
-    def layer(m, carry):
-        @pl.when(section > 0)
+    def attend(m, carry):
+        @pl.when((section > 0) & jnp.logical_not(takes))
         def _():
             pass_on(m).wait_recv()
+
+        if giver >= 0:
+            @pl.when(takes)
+            def _():
+                skip_copy(m).wait_recv()
+                mixed_copy(m).wait_recv()
+                for start in range(0, width, 256):
+                    stop = min(start + 256, width)
+                    x_in[m, :, start:stop] = (
+                        x_before[m, :, start:stop].astype(jnp.float32)
+                        + jnp.dot(mixed_in[m], w_before[:, start:stop], preferred_element_type=jnp.float32)
+                    ).astype(jnp.bfloat16)
 
         live = live_row(m)
         tokens = x_in[m].astype(jnp.float32)
@@ -212,23 +282,39 @@
             proj[:, start:stop] = jnp.dot(
                 normed, w_qkv[:, start:stop], preferred_element_type=jnp.float32
             ).astype(jnp.bfloat16)
-        context[...] = jnp.zeros_like(context)
-        for head in range(HEADS):
+        tiles = [(head * HDIM // 128 * 128, -(-(head + 1) * HDIM // 128) * 128) for head in range(HEADS)]
+        insides, scored = [], []
+        for head, (left, right) in enumerate(tiles):
             low, high = head * HDIM, (head + 1) * HDIM
-            left, right = low // 128 * 128, -(-high // 128) * 128
             lane = lax.broadcasted_iota(jnp.int32, (1, right - left), 1) + left
             inside = jnp.where((lane >= low) & (lane < high), 1.0, 0.0).astype(jnp.bfloat16)
-            queries = proj[:, left:right] * inside
-            key_rows = proj[:, head_width + left:head_width + right]
-            value_rows = proj[:, 2 * head_width + left:2 * head_width + right] * inside
+            insides.append(inside)
             scores = lax.dot_general(
-                queries, key_rows, (((1,), (1,)), ((), ())), preferred_element_type=jnp.float32
+                proj[:, left:right] * inside, proj[:, head_width + left:head_width + right],
+                (((1,), (1,)), ((), ())), preferred_element_type=jnp.float32,
             ) * HDIM ** (-0.5)
-            scores = jnp.where(live, scores, -1e30)
-            weights = jnp.exp(scores - jnp.max(scores, -1, keepdims=True))
-            shares = (weights / jnp.sum(weights, -1, keepdims=True)).astype(jnp.bfloat16)
-            context[:, left:right] += jnp.dot(shares, value_rows, preferred_element_type=jnp.float32)
-        mixed = context[...].astype(jnp.bfloat16)
+            scored.append(jnp.where(live, scores, -1e30))
+        peaks = [jnp.max(scores, -1, keepdims=True) for scores in scored]
+        grown = [jnp.exp(scores - peak) for scores, peak in zip(scored, peaks)]
+        totals = [jnp.sum(weights, -1, keepdims=True) for weights in grown]
+        shares = [(weights / total).astype(jnp.bfloat16) for weights, total in zip(grown, totals)]
+        columns = [None] * (head_width // 128)
+        for head, (left, right) in enumerate(tiles):
+            part = jnp.dot(
+                shares[head], proj[:, 2 * head_width + left:2 * head_width + right] * insides[head],
+                preferred_element_type=jnp.float32,
+            )
+            for tile in range(left // 128, right // 128):
+                piece = part[:, tile * 128 - left:tile * 128 - left + 128]
+                columns[tile] = piece if columns[tile] is None else columns[tile] + piece
+        for tile, piece in enumerate(columns):
+            mixed_all[m, :, tile * 128:tile * 128 + 128] = piece.astype(jnp.bfloat16)
+        if giver >= 0:
+            pl.when(gives)(mixed_copy(m).start)
+        return carry
+
+    def output(m, carry):
+        mixed = mixed_all[m]
         for start in range(0, width, 256):
             stop = min(start + 256, width)
             x_out[m, :, start:stop] = (
@@ -236,10 +322,13 @@
                 + jnp.dot(mixed, w_out[:, start:stop], preferred_element_type=jnp.float32)
             ).astype(jnp.bfloat16)
 
-        @pl.when(section < sections - 1)
-        def _():
-            pass_on(m).start()
-
+        pl.when(passes)(pass_on(m).start)
+        if giver > 0:
+            pl.when(section == giver - 1)(skip_copy(m).start)
+        return carry
+
+    def report(m, carry):
+        live = live_row(m)
         output = x_out[m].astype(jnp.float32)
         live_value = jnp.where(live, 1.0, 0.0)
         live_column = to_column(live_value, rows) > 0.5
@@ -253,7 +342,23 @@
         )
         return carry
 
-    lax.fori_loop(0, micro_count, layer, 0)
+    def both(m, carry):
+        return output(m, attend(m, carry))
+
+    @pl.when(gives)
+    def _():
+        lax.fori_loop(0, micro_count, attend, 0)
+        lax.fori_loop(0, micro_count, output, 0)
+        lax.fori_loop(0, micro_count, report, 0)
+
+    @pl.when(section == sections - 1)
+    def _():
+        lax.fori_loop(0, micro_count, lambda m, carry: report(m, both(m, carry)), 0)
+
+    @pl.when((section < sections - 1) & jnp.logical_not(gives))
+    def _():
+        lax.fori_loop(0, micro_count, both, 0)
+        lax.fori_loop(0, micro_count, report, 0)
 
     def error_copy(distance, slot, peer):
         return pltpu.make_async_remote_copy(
@@ -303,10 +408,27 @@
     for m in range(micro_count):
         pltpu.make_async_copy(hidden_held.at[m], hidden.at[m], hidden_sem.at[m]).wait()
 
-    @pl.when(section < sections - 1)
+    @pl.when(passes)
     def _():
         for m in range(micro_count):
             pass_on(m).wait_send()
+
+    if giver >= 0:
+        @pl.when(takes)
+        def _():
+            for step, p, way in relayed:
+                hop(way, step, 2, p, device_at(place - (1 - 2 * way) * step)).wait_send()
+
+        @pl.when(gives)
+        def _():
+            before_copy().wait_send()
+            for m in range(micro_count):
+                mixed_copy(m).wait_send()
+
+        @pl.when(section == giver - 1)
+        def _():
+            for m in range(micro_count):
+                skip_copy(m).wait_send()
 
 
 def per_device(
@@ -315,7 +437,7 @@
     sections, ring_size = lax.axis_size("section"), lax.axis_size("dp")
     micro_count, _, slots = visible.shape
     patch_count, width = patch_tokens.shape[2:]
-    rows = -(-slots // 16) * 16
+    rows = slots
     w_qkv, w_out = qkv_weight[0], out_weight[0]
     gathers = ring_size % 2 == 0 and w_qkv.shape[0] % 32 == 0 and w_out.shape[0] % 16 == 0
     if not gathers:
@@ -350,8 +472,8 @@
             pltpu.VMEM((2 * micro_count, 1, 128), jnp.float32),
             pltpu.VMEM((ring_size, 2 * micro_count, 1, 128), jnp.float32),
             dma((2,)),
-            dma((4 * ring_size,)),
-            dma((4 * ring_size,)),
+            dma((6 * ring_size,)),
+            dma((6 * ring_size,)),
             dma((micro_count,)),
             dma((micro_count,)),
             dma((sections,)),
@@ -366,6 +488,16 @@
             pltpu.VMEM((micro_count, patch_count, width), jnp.bfloat16),
             dma,
             pltpu.VMEM((micro_count, slots, width), jnp.bfloat16),
+            dma((micro_count,)),
+            pltpu.VMEM(full_out, jnp.bfloat16),
+            pltpu.VMEM((micro_count, rows, HEADS * HDIM), jnp.bfloat16),
+            pltpu.VMEM((micro_count, rows, HEADS * HDIM), jnp.bfloat16),
+            pltpu.VMEM((micro_count, rows, width), jnp.bfloat16),
+            dma,
+            dma,
+            dma((micro_count,)),
+            dma((micro_count,)),
+            dma((micro_count,)),
             dma((micro_count,)),
         ],
         compiler_params=pltpu.CompilerParams(

time: 105 us -> 102 us (0.971)
  Pallas kernels: 100 us -> 97.5 us
    pallas_call x1, Pallas kernels: 100 us -> 97.5 us  [per_device(): pl.pallas_call(functools.partial(kernel_body, gathers, sections, ring_siz...]
where the time goes in v2:
time: 102 us
  Pallas kernels  97.5 us (96%)
  local copies, waits for them, and re-layouts  3.78 us (4%)
    pallas_call x1, Pallas kernels, per_device(): pl.pallas_call(functools.partial(kernel_body, gathers, sections, ring_siz...  97.5 us
    unnamed x6, local copies, waits for them, and re-layouts  3.16 us

profile of v2, /device:TPU:0, one launch (start us, length us, event | category | flops | bytes accessed | tf_op | source)
XLA Modules:
  0.0 101.9 jit_solution(627850982235487197)
XLA Ops:
  0.6 97.5 %shard_map.103 = (bf16[4,98,1280]{2,1,0:T(8,128)(2,1)}, f32[4,1,98]{2,1,0:T(1,128)}, f32[4,1,128]{2,1,0:T(1,128)}) custom-call(s32[4]{0:T(128)} %lengths.1, bf16[196,4,1280]{2,1,0:T(4,128)(2,1)} %bitcast.9, s32[4,1,98]{2,1,0:T(1,128)} %visible.1, s32[4,1,98]{2,1,0:T(1,128)} %keep.1, bf16[160,1920]{1,0:T(8,128)(2,1)} %bitcast.12, bf16[80,1280]{1,0:T(8,128)(2,1)} %bitcast.13, ...), custom_call_target="tpu_custom_call" | custom-call | tf_op jit(solution)/shard_map/pallas_call | solution.py:452
  98.1 0.0 copy-start
  98.2 0.0 copy-start.1
  98.2 2.6 %copy.12 = bf16[1,4,1,98,1280]{4,1,3,2,0:T(4,128)(2,1)} copy(bf16[1,4,1,98,1280]{4,3,1,2,0:T(8,128)(2,1)} %bitcast.10) | data formatting | bytes 2007040
  100.7 0.0 copy-done
  100.7 0.6 slice_reduce_fusion
  101.4 0.0 copy-done.1
  101.4 0.6 copy.14
Async XLA Ops:
  98.1 2.6 %copy-start = (f32[4,1,128]{2,1,0:T(1,128)S(1)}, f32[4,1,128]{2,1,0:T(1,128)}, u32[]{:S(2)}) copy-start(f32[4,1,128]{2,1,0:T(1,128)} %get-tuple-element.8) | copy-start | bytes 6148
  98.2 3.2 %copy-start.1 = (f32[4,1,98]{2,1,0:T(1,128)S(1)}, f32[4,1,98]{2,1,0:T(1,128)}, u32[]{:S(2)}) copy-start(f32[4,1,98]{2,1,0:T(1,128)} %get-tuple-element.19) | copy-start | bytes 4708

commit v3 on v2

--- a/solution.py
+++ b/solution.py
@@ -54,13 +54,13 @@
     width = x_in.shape[2]
     head_width = HEADS * HDIM
 
-    pairs = ((w_qkv_in, w_qkv_all), (w_out_in, w_out_all), (w_out_in, w_before))
+    pairs = ((w_qkv_in, w_qkv_all), (w_out_in, w_out_all))
     giver = sections // 2 - 1 if gathers and sections % 2 == 0 and sections >= 4 else -2
     taker = giver + 1
     gives, takes = section == giver, section == taker
     own_copies = []
     if gathers:
-        for which, (shard, whole) in enumerate(pairs[:2]):
+        for which, (shard, whole) in enumerate(pairs):
             own_rows = shard.shape[0]
             target = whole.at[pl.ds(pl.multiple_of(member * own_rows, 16), own_rows)]
             own_copies.append(pltpu.make_async_copy(shard, target, own_sem.at[which]))
@@ -103,6 +103,13 @@
             device_id={"section": taker}, device_id_type=MESH,
         )
 
+    def share_copy(there):
+        return pltpu.make_async_remote_copy(
+            src_ref=w_out_all.at[there], dst_ref=w_before.at[there],
+            send_sem=before_send, recv_sem=before_recv,
+            device_id={"section": taker}, device_id_type=MESH,
+        )
+
     if giver >= 0:
         @pl.when(gives)
         def _():
@@ -136,7 +143,7 @@
             lax.fori_loop(0, micro_count, pick, 0)
 
     if gathers:
-        pieces = [(which, part) for part in (0, 1) for which in (0, 1)]
+        pieces = [(which, part) for which in (1, 0) for part in (0, 1)]
 
         def span(which, part, owner):
             shard_rows = pairs[which][0].shape[0]
@@ -145,7 +152,7 @@
 
         def hop(way, step, which, part, owner):
             there = pairs[which][1].at[span(which, part, owner)]
-            index = ((way * half + step) * 3 + which) * 2 + part
+            index = ((way * half + step) * 2 + which) * 2 + part
             return pltpu.make_async_remote_copy(
                 src_ref=there, dst_ref=there,
                 send_sem=ring_send.at[index], recv_sem=ring_recv.at[index],
@@ -198,33 +205,10 @@
                         copy = hop(way, step + 1, w, p, owner)
                         copy.start()
                         started.append(copy)
-        relayed = []
-        if giver >= 0:
-            before = [
-                hop(way, 0, 2, p, member)
-                for p in (0, 1) for way in (0, 1) if (1, p) in wanted(way, 0)
-            ]
-            relayed.extend((0, p, way) for p in (0, 1) for way in (0, 1) if (1, p) in wanted(way, 0))
-
-            @pl.when(takes)
-            def _():
-                before_copy().wait_recv()
-                for copy in before:
-                    copy.start()
-                for step in range(half):
-                    for p in (0, 1):
-                        for way in (0, 1):
-                            if (1, p) not in wanted(way, step):
-                                continue
-                            owner = device_at(place - (1 - 2 * way) * (step + 1))
-                            hop(way, step, 2, p, owner).wait_recv()
-                            if step + 1 < half and (1, p) in wanted(way, step + 1):
-                                hop(way, step + 1, 2, p, owner).start()
-                                relayed.append((step + 1, p, way))
-
+                    if w == 1 and giver >= 0:
+                        pl.when(gives)(share_copy(span(1, p, owner)).start)
         w_qkv, w_out = w_qkv_all, w_out_all
     else:
-        relayed = []
         prepare()
         started = []
         w_qkv, w_out = w_qkv_in, w_out_in
@@ -345,6 +329,11 @@
     def both(m, carry):
         return output(m, attend(m, carry))
 
+    if giver >= 0:
+        @pl.when(takes)
+        def _():
+            share_copy(pl.ds(0, w_before.shape[0])).wait_recv()
+
     @pl.when(gives)
     def _():
         lax.fori_loop(0, micro_count, attend, 0)
@@ -414,14 +403,9 @@
             pass_on(m).wait_send()
 
     if giver >= 0:
-        @pl.when(takes)
-        def _():
-            for step, p, way in relayed:
-                hop(way, step, 2, p, device_at(place - (1 - 2 * way) * step)).wait_send()
-
         @pl.when(gives)
         def _():
-            before_copy().wait_send()
+            share_copy(pl.ds(0, w_before.shape[0])).wait_send()
             for m in range(micro_count):
                 mixed_copy(m).wait_send()
 
@@ -472,8 +456,8 @@
             pltpu.VMEM((2 * micro_count, 1, 128), jnp.float32),
             pltpu.VMEM((ring_size, 2 * micro_count, 1, 128), jnp.float32),
             dma((2,)),
-            dma((6 * ring_size,)),
-            dma((6 * ring_size,)),
+            dma((4 * ring_size,)),
+            dma((4 * ring_size,)),
             dma((micro_count,)),
             dma((micro_count,)),
             dma((sections,)),

time: 102 us -> 102 us (level)
  no operation moved by 1% of the time
where the time goes in v3:
time: 102 us
  Pallas kernels  97.2 us (95%)
  local copies, waits for them, and re-layouts  3.78 us (4%)
    pallas_call x1, Pallas kernels, per_device(): pl.pallas_call(functools.partial(kernel_body, gathers, sections, ring_siz...  97.2 us
    unnamed x6, local copies, waits for them, and re-layouts  3.16 us

profile of v3, /device:TPU:0, one launch (start us, length us, event | category | flops | bytes accessed | tf_op | source)
XLA Modules:
  0.0 101.6 jit_solution(13186056130235166025)
XLA Ops:
  0.6 97.2 %shard_map.103 = (bf16[4,98,1280]{2,1,0:T(8,128)(2,1)}, f32[4,1,98]{2,1,0:T(1,128)}, f32[4,1,128]{2,1,0:T(1,128)}) custom-call(s32[4]{0:T(128)} %lengths.1, bf16[196,4,1280]{2,1,0:T(4,128)(2,1)} %bitcast.9, s32[4,1,98]{2,1,0:T(1,128)} %visible.1, s32[4,1,98]{2,1,0:T(1,128)} %keep.1, bf16[160,1920]{1,0:T(8,128)(2,1)} %bitcast.12, bf16[80,1280]{1,0:T(8,128)(2,1)} %bitcast.13, ...), custom_call_target="tpu_custom_call" | custom-call | tf_op jit(solution)/shard_map/pallas_call | solution.py:436
  97.8 0.0 copy-start
  97.9 0.0 copy-start.1
  97.9 2.6 %copy.12 = bf16[1,4,1,98,1280]{4,1,3,2,0:T(4,128)(2,1)} copy(bf16[1,4,1,98,1280]{4,3,1,2,0:T(8,128)(2,1)} %bitcast.10) | data formatting | bytes 2007040
  100.4 0.0 copy-done
  100.4 0.6 slice_reduce_fusion
  101.1 0.0 copy-done.1
  101.1 0.6 copy.14
Async XLA Ops:
  97.8 2.6 %copy-start = (f32[4,1,128]{2,1,0:T(1,128)S(1)}, f32[4,1,128]{2,1,0:T(1,128)}, u32[]{:S(2)}) copy-start(f32[4,1,128]{2,1,0:T(1,128)} %get-tuple-element.8) | copy-start | bytes 6148
  97.9 3.2 %copy-start.1 = (f32[4,1,98]{2,1,0:T(1,128)S(1)}, f32[4,1,98]{2,1,0:T(1,128)}, u32[]{:S(2)}) copy-start(f32[4,1,98]{2,1,0:T(1,128)} %get-tuple-element.19) | copy-start | bytes 4708
